TPU v7x, 32 devices: a whole 2x2x4 slice. The times are simulated.
32 devices in a mesh: cache: 4 (over x, core), expert: 8 (over z, y).
Axes of the slice: x: 2, y: 2, z: 4, core: 2. Of those that a mesh axis runs over, the one named last changes fastest.
Arguments:
- queries: bfloat16 [2, 32, 2048], P(None, 'expert'), may hold values from -16 to 16
- k_cache: bfloat16 [32, 4096, 256], P('expert', 'cache'), may hold values from -6 to 6
- v_cache: bfloat16 [32, 4096, 256], P('expert', 'cache'), may hold values from -6 to 6
- lengths: int32 [32], P('expert'), may hold values from 1 to 4094
- w_out: bfloat16 [2048, 2880], P('cache'), may hold values from -0.125 to 0.125
- norm_gain: float32 [2880], replicated, may hold values from 0.25 to 1.75
- w_gate: bfloat16 [8, 2880, 1440], P('cache', 'expert'), may hold values from -0.109375 to 0.109375
- w_up: bfloat16 [8, 2880, 1440], P('cache', 'expert'), may hold values from -0.109375 to 0.109375
- w_down: bfloat16 [8, 1440, 2880], P('cache', None, 'expert'), may hold values from -0.15625 to 0.15625
- expert_ids: int32 [2, 32, 4], P(None, 'expert'), may hold values from 0 to 7, all different within a row; in each aligned block of 4 rows (0 to 3, 4 to 7, ..., all dimensions but the last counted through in order) at most 2 rows name the same one
- gate_weights: float32 [2, 32, 4], P(None, 'expert'), may hold values from 0.1 to 1
Outputs:
- mixed: bfloat16 [2, 32, 2880], P(None, 'expert')
- gate_owner: bfloat16 [8, 2880, 1440], P('expert', None, 'cache')
- up_owner: bfloat16 [8, 2880, 1440], P('expert', None, 'cache')
- down_owner: bfloat16 [8, 1440, 2880], P('expert', 'cache')
Inputs may be any that keep to these rules, and one draw needn't show every extreme that they name: `expert_ids`: in each step the 4 rows of one index of expert name one expert at most 2 times; a row names 4 different experts.
All inputs are finite; a program needn't handle non-finite values.
Results may differ from a plain program's by a relative error of at most 0.015.
Values may be sent and summed in bfloat16 or wider, within the bound.
A program may use at most 64 MiB of HBM per device.

v0:
```python
import math

import jax
import jax.numpy as jnp
from jax import lax
from jax.sharding import PartitionSpec as P

D = 2880
QH = 32
KVH = 4
HD = 64
TOP = 4


def joined(part, axis, combine):
    gathered = jax.tree.map(lambda a: lax.all_gather(a, axis), part)

    def take(source):
        return jax.tree.map(lambda a: lax.dynamic_index_in_dim(a, source, 0, False), gathered)

    return lax.fori_loop(
        1, lax.axis_size(axis), lambda source, state: combine(state, take(source)), take(0)
    )


def merge_partials(first, second):
    first_high, first_mass, first_accum = first
    second_high, second_mass, second_accum = second
    shared = jnp.maximum(first_high, second_high)
    first_factor = jnp.exp(first_high - shared)
    second_factor = jnp.exp(second_high - shared)
    head_width = first_accum.shape[-1] // first_high.shape[-1]
    accum = first_accum * jnp.repeat(first_factor, head_width, axis=-1) + second_accum * jnp.repeat(
        second_factor, head_width, axis=-1
    )
    return (shared, first_mass * first_factor + second_mass * second_factor, accum)


def shards(
    queries,
    k_cache,
    v_cache,
    lengths,
    w_out,
    norm_gain,
    w_gate,
    w_up,
    w_down,
    expert_ids,
    gate_weights,
):
    gate_owner, up_owner = (
        lax.all_to_all(
            lax.all_to_all(w_gate, "cache", split_axis=2, concat_axis=0, tiled=True),
            "expert",
            split_axis=0,
            concat_axis=1,
            tiled=True,
        ),
        lax.all_to_all(
            lax.all_to_all(w_up, "cache", split_axis=2, concat_axis=0, tiled=True),
            "expert",
            split_axis=0,
            concat_axis=1,
            tiled=True,
        ),
    )
    down_owner = lax.all_to_all(
        lax.all_to_all(w_down, "cache", split_axis=1, concat_axis=0, tiled=True),
        "expert",
        split_axis=0,
        concat_axis=2,
        tiled=True,
    )
    cache_count = lax.axis_size("cache")
    cache_place = lax.axis_index("cache")
    step_count = queries.shape[0]
    row_count = k_cache.shape[0]
    positions = k_cache.shape[1]
    group_size = QH // KVH
    query_heads = queries.reshape(step_count, row_count, KVH, group_size, HD)
    key_heads = k_cache.reshape(row_count, positions, KVH, HD)
    value_heads = v_cache.reshape(row_count, positions, KVH, HD)
    scores = jnp.einsum(
        "srhgd,rphd->srhgp", query_heads, key_heads, preferred_element_type=jnp.float32
    ) * (1.0 / math.sqrt(HD))
    position = cache_place * positions + jnp.arange(positions, dtype=jnp.int32)
    limit = lengths[None, :] + jnp.arange(step_count, dtype=jnp.int32)[:, None] + 1
    visible = (position[None, None, :] < limit[:, :, None])[:, :, None, None, :]
    highest = jnp.max(jnp.where(visible, scores, -1e30), axis=-1)
    weights = jnp.where(visible, jnp.exp(scores - highest[..., None]), 0.0)
    mass = jnp.sum(weights, axis=-1).reshape(step_count, row_count, QH)
    accum = jnp.einsum(
        "srhgp,rphd->srhgd",
        weights.astype(jnp.bfloat16),
        value_heads,
        preferred_element_type=jnp.float32,
    )
    accum = accum.reshape(step_count, row_count, QH * HD)
    highest = highest.reshape(step_count, row_count, QH)
    own_width = w_out.shape[0]
    all_high, all_mass, all_accum = joined((highest, mass, accum), "cache", merge_partials)
    heads_out = all_accum / jnp.repeat(all_mass, HD, axis=-1)
    own_out = lax.dynamic_slice_in_dim(heads_out, cache_place * own_width, own_width, 2)
    own_rows = own_out.astype(jnp.bfloat16).reshape(step_count * row_count, own_width)
    projected = jnp.dot(own_rows, w_out, preferred_element_type=jnp.float32)
    attention = lax.psum(projected, "cache")
    scale = lax.rsqrt(jnp.mean(attention * attention, axis=-1, keepdims=True) + 1e-05)
    normed = (attention * scale * norm_gain).astype(jnp.bfloat16).reshape(step_count, row_count, D)
    experts_total = w_gate.shape[0] * cache_count
    capacity = max(2, (row_count * TOP + experts_total - 1) // experts_total)
    expert_range = jnp.arange(experts_total, dtype=jnp.int32)
    onehot = (expert_ids[..., None] == expert_range).astype(jnp.float32)
    chosen = jnp.sum(onehot, axis=2)
    gate_map = jnp.sum(onehot * gate_weights[..., None], axis=2)
    earlier = jnp.tril(jnp.ones((row_count, row_count), jnp.float32), -1)
    ranks = jnp.einsum("rq,sqe->sre", earlier, chosen, precision=lax.Precision.HIGHEST)
    slot_table = (ranks[..., None] == jnp.arange(capacity, dtype=jnp.float32)).astype(
        jnp.float32
    ) * chosen[..., None]
    outgoing = jnp.einsum(
        "srec,srd->escd",
        slot_table.astype(jnp.bfloat16),
        normed,
        preferred_element_type=jnp.float32,
    )
    outgoing = outgoing.astype(jnp.bfloat16).reshape(experts_total, step_count * capacity, D)
    slots = lax.all_to_all(outgoing, "expert", split_axis=0, concat_axis=0, tiled=True)
    source_count = slots.shape[0]
    item_count = slots.shape[1]
    slot_rows = slots.reshape(source_count * item_count, D)
    gate_value = jnp.dot(slot_rows, gate_owner[0], preferred_element_type=jnp.float32)
    up_value = jnp.dot(slot_rows, up_owner[0], preferred_element_type=jnp.float32)
    hidden = (jax.nn.silu(gate_value) * up_value).astype(jnp.bfloat16)
    partial_out = jnp.dot(hidden, down_owner[0], preferred_element_type=jnp.float32).reshape(
        source_count, item_count, D
    )
    expert_out = lax.psum(partial_out, "cache").astype(jnp.bfloat16)
    returned = lax.all_to_all(expert_out, "expert", split_axis=0, concat_axis=0, tiled=True)
    back_width = returned.shape[-1]
    returned = returned.reshape(experts_total, step_count, capacity, back_width)
    combined = jnp.einsum(
        "srec,escd->srd",
        slot_table * gate_map[..., None],
        returned.astype(jnp.float32),
        precision=lax.Precision.HIGHEST,
    )
    attention_rows = attention.reshape(step_count, row_count, D)
    mixed = (attention_rows + combined).astype(jnp.bfloat16)
    return (mixed, gate_owner, up_owner, down_owner)


def solution(mesh):
    return jax.shard_map(
        shards,
        mesh=mesh,
        in_specs=(
            P(None, "expert", None),
            P("expert", "cache", None),
            P("expert", "cache", None),
            P("expert"),
            P("cache", None),
            P(),
            P("cache", "expert", None),
            P("cache", "expert", None),
            P("cache", None, "expert"),
            P(None, "expert", None),
            P(None, "expert", None),
        ),
        out_specs=(
            P(None, "expert", None),
            P("expert", None, "cache"),
            P("expert", None, "cache"),
            P("expert", "cache", None),
        ),
        check_vma=False,
    )
```

profile of v0, /device:TPU:0, one launch (start us, length us, event | category | flops | bytes accessed | tf_op | source)
XLA Modules:
  0.0 412.6 jit_solution(15657608075601051097)
XLA Ops:
  7.2 0.9 add_add_fusion
  9.0 4.0 copy.74
  13.0 2.1 select_reduce_fusion
  15.1 0.9 copy-done.2
  16.5 6.7 %all_gather.10 = f32[4,2,4,32]{3,2,1,0:T(4,128)} all-gather(f32[1,2,4,32]{3,2,1,0:T(4,128)S(1)} %all_gather_reshape.10), channel_id=1, replica_groups=mesh['cache'=4,'expert'=8] {'cache'}, dimensions={0}, use_global_device_ids=true | all-gather | bytes 5120 | tf_op jit(solution)/shard_map/all_gather | solution.py:16
  24.0 5.8 %all_gather.9 = f32[4,2,4,32]{3,2,1,0:T(4,128)} all-gather(f32[1,2,4,32]{3,2,1,0:T(4,128)S(1)} %all_gather_reshape.9), channel_id=1, replica_groups=mesh['cache'=4,'expert'=8] {'cache'}, dimensions={0}, use_global_device_ids=true | all-gather | bytes 5120 | tf_op jit(solution)/shard_map/all_gather | solution.py:16
  30.5 3.9 copy.78
  34.4 2.6 convolution_bitcast_fusion.1
  37.2 6.0 %all_gather.11 = f32[4,2,4,2048]{3,2,1,0:T(4,128)S(1)} all-gather(f32[1,2,4,2048]{3,2,1,0:T(4,128)S(1)} %all_gather_reshape.11), channel_id=1, replica_groups=mesh['cache'=4,'expert'=8] {'cache'}, dimensions={0}, use_global_device_ids=true | all-gather | bytes 327680 | tf_op jit(solution)/shard_map/all_gather | solution.py:16
  43.2 3.6 while.19
  47.0 1.5 fusion.36
  48.9 32.8 %all-reduce.3.cloned.1.call-done = f32[8,2880]{1,0:T(8,128)} async-done(((f32[8,2880]{1,0:T(8,128)}), f32[8,2880]{1,0:T(8,128)}) %all-reduce.3.cloned.1.call-update) | async-done | bytes 92176 | tf_op jit(solution)/shard_map/psum | solution.py:107
  81.7 1.0 multiply_reduce_fusion
  82.8 1.0 multiply_convert_fusion
  84.8 5.5 %all-to-all-start = ((bf16[8,4,2880]{2,1,0:T(4,128)(2,1)}), bf16[8,4,2880]{2,1,0:T(4,128)(2,1)S(1)}, u32[]{:S(2)}, u32[]{:S(2)}) async-start(bf16[8,4,2880]{2,1,0:T(4,128)(2,1)} %copy.80), calls=%async_computation | async-start | bytes 376832 | tf_op jit(solution)/shard_map/all_to_all | solution.py:128
  90.3 6.8 %copy.81 = bf16[2,360,1440]{1,0,2:T(2,128)(2,1)} copy(bf16[2,360,1440]{2,1,0:T(8,128)(2,1)} %param.19) | data formatting | bytes 4147200 | tf_op args[6]
  97.1 0.9 all-to-all-done
  98.0 4.5 %all-to-all-start.1 = ((bf16[2,360,1440]{1,0,2:T(2,128)(2,1)}), bf16[2,360,1440]{1,0,2:T(2,128)(2,1)}, u32[]{:S(2)}, u32[]{:S(2)}) async-start(bf16[2,360,1440]{1,0,2:T(2,128)(2,1)} %copy.81), calls=%async_computation.1 | async-start | bytes 4423680 | tf_op jit(solution)/shard_map/all_to_all | solution.py:54
  102.5 6.8 %copy.84 = bf16[2,360,1440]{1,0,2:T(2,128)(2,1)} copy(bf16[2,360,1440]{2,1,0:T(8,128)(2,1)} %param.20) | data formatting | bytes 4147200 | tf_op args[7]
  109.3 20.2 %all-to-all-done.1 = bf16[2,360,1440]{1,0,2:T(2,128)(2,1)} async-done(((bf16[2,360,1440]{1,0,2:T(2,128)(2,1)}), bf16[2,360,1440]{1,0,2:T(2,128)(2,1)}, u32[]{:S(2)}, u32[]{:S(2)}) %all-to-all-start.1) | async-done | bytes 2073632 | tf_op jit(solution)/shard_map/all_to_all | solution.py:54
  129.5 4.5 %all-to-all-start.3 = ((bf16[2,360,1440]{1,0,2:T(2,128)(2,1)}), bf16[2,360,1440]{1,0,2:T(2,128)(2,1)}, u32[]{:S(2)}, u32[]{:S(2)}) async-start(bf16[2,360,1440]{1,0,2:T(2,128)(2,1)} %copy.84), calls=%async_computation.3 | async-start | bytes 4423680 | tf_op jit(solution)/shard_map/all_to_all | solution.py:61
  134.0 12.9 %copy.87 = bf16[2,1440,360]{2,0,1:T(2,128)(2,1)} copy(bf16[2,1440,360]{2,1,0:T(8,128)(2,1)} %param.21) | data formatting | bytes 4147200 | tf_op args[8]
  146.9 14.0 %all-to-all-done.3 = bf16[2,360,1440]{1,0,2:T(2,128)(2,1)} async-done(((bf16[2,360,1440]{1,0,2:T(2,128)(2,1)}), bf16[2,360,1440]{1,0,2:T(2,128)(2,1)}, u32[]{:S(2)}, u32[]{:S(2)}) %all-to-all-start.3) | async-done | bytes 2073632 | tf_op jit(solution)/shard_map/all_to_all | solution.py:61
  160.9 4.5 %all-to-all-start.5 = ((bf16[2,1440,360]{2,0,1:T(2,128)(2,1)}), bf16[2,1440,360]{2,0,1:T(2,128)(2,1)}, u32[]{:S(2)}, u32[]{:S(2)}) async-start(bf16[2,1440,360]{2,0,1:T(2,128)(2,1)} %copy.87), calls=%async_computation.5 | async-start | bytes 4423680 | tf_op jit(solution)/shard_map/all_to_all | solution.py:69
  165.4 3.3 copy.82
  168.7 23.6 %all-to-all-done.5 = bf16[2,1440,360]{2,0,1:T(2,128)(2,1)} async-done(((bf16[2,1440,360]{2,0,1:T(2,128)(2,1)}), bf16[2,1440,360]{2,0,1:T(2,128)(2,1)}, u32[]{:S(2)}, u32[]{:S(2)}) %all-to-all-start.5) | async-done | bytes 2073632 | tf_op jit(solution)/shard_map/all_to_all | solution.py:69
  192.3 5.1 %all-to-all-start.2 = ((bf16[8,360,360]{1,2,0:T(8,128)(2,1)}), bf16[8,360,360]{1,2,0:T(8,128)(2,1)}, u32[]{:S(2)}, u32[]{:S(2)}) async-start(bf16[8,360,360]{1,2,0:T(8,128)(2,1)} %bitcast.104), calls=%async_computation.2 | async-start | bytes 4423680 | tf_op jit(solution)/shard_map/all_to_all | solution.py:53
  197.4 3.4 copy.85
  200.8 47.1 %all-to-all-done.2 = bf16[8,360,360]{1,2,0:T(8,128)(2,1)} async-done(((bf16[8,360,360]{1,2,0:T(8,128)(2,1)}), bf16[8,360,360]{1,2,0:T(8,128)(2,1)}, u32[]{:S(2)}, u32[]{:S(2)}) %all-to-all-start.2) | async-done | bytes 2073632 | tf_op jit(solution)/shard_map/all_to_all | solution.py:53
  247.9 4.4 %all-to-all-start.4 = ((bf16[8,360,360]{1,2,0:T(8,128)(2,1)}), bf16[8,360,360]{1,2,0:T(8,128)(2,1)}, u32[]{:S(2)}, u32[]{:S(2)}) async-start(bf16[8,360,360]{1,2,0:T(8,128)(2,1)} %bitcast.105), calls=%async_computation.4 | async-start | bytes 4423680 | tf_op jit(solution)/shard_map/all_to_all | solution.py:60
  252.3 3.3 copy.88
  255.6 46.9 %all-to-all-done.4 = bf16[8,360,360]{1,2,0:T(8,128)(2,1)} async-done(((bf16[8,360,360]{1,2,0:T(8,128)(2,1)}), bf16[8,360,360]{1,2,0:T(8,128)(2,1)}, u32[]{:S(2)}, u32[]{:S(2)}) %all-to-all-start.4) | async-done | bytes 2073632 | tf_op jit(solution)/shard_map/all_to_all | solution.py:60
  302.6 4.5 %all-to-all-start.6 = ((bf16[8,360,360]{2,1,0:T(8,128)(2,1)}), bf16[8,360,360]{2,1,0:T(8,128)(2,1)}, u32[]{:S(2)}, u32[]{:S(2)}) async-start(bf16[8,360,360]{2,1,0:T(8,128)(2,1)} %bitcast.103), calls=%async_computation.6 | async-start | bytes 4423680 | tf_op jit(solution)/shard_map/all_to_all | solution.py:68
  307.2 4.2 %copy.83 = bf16[8,360,360]{2,1,0:T(8,128)(2,1)} copy(bf16[8,360,360]{1,2,0:T(8,128)(2,1)} %all-to-all-done.2) | data formatting | bytes 4147200 | tf_op jit(solution)/shard_map/all_to_all | solution.py:53
  311.4 4.2 %copy.86 = bf16[8,360,360]{2,1,0:T(8,128)(2,1)} copy(bf16[8,360,360]{1,2,0:T(8,128)(2,1)} %all-to-all-done.4) | data formatting | bytes 4147200 | tf_op jit(solution)/shard_map/all_to_all | solution.py:60
  315.6 2.2 fusion.37
  318.4 38.9 %all-to-all-done.6 = bf16[8,360,360]{2,1,0:T(8,128)(2,1)} async-done(((bf16[8,360,360]{2,1,0:T(8,128)(2,1)}), bf16[8,360,360]{2,1,0:T(8,128)(2,1)}, u32[]{:S(2)}, u32[]{:S(2)}) %all-to-all-start.6) | async-done | bytes 2073632 | tf_op jit(solution)/shard_map/all_to_all | solution.py:68
  357.3 3.3 copy.89
  360.6 4.8 %reshape.124 = bf16[360,2880,1]{1,0,2:T(8,128)(2,1)} reshape(bf16[1,360,8,360]{3,2,1,0:T(8,128)(2,1)} %copy.89) | data formatting | bytes 4147200 | tf_op jit(solution)/shard_map/squeeze | solution.py:135
  365.4 2.0 fusion.15
  367.5 14.8 %all-reduce.4 = bf16[8,4,2880]{2,0,1:T(8,128)(2,1)} all-reduce(f32[8,4,2880]{2,0,1:T(8,128)S(1)} %fusion.15), channel_id=1, replica_groups=mesh['cache'=4,'expert'=8] {'cache'}, use_global_device_ids=true, to_apply=%region_8.9 | all-reduce | flops 92160 | bytes 552960 | tf_op jit(solution)/shard_map/psum | solution.py:138
  382.2 1.7 copy.91
  383.9 4.3 %all-to-all-start.7 = ((bf16[8,4,2880]{2,1,0:T(4,128)(2,1)}), bf16[8,4,2880]{2,1,0:T(4,128)(2,1)S(1)}, u32[]{:S(2)}, u32[]{:S(2)}) async-start(bf16[8,4,2880]{2,1,0:T(4,128)(2,1)} %copy.91), calls=%async_computation.7 | async-start | bytes 376832 | tf_op jit(solution)/shard_map/all_to_all | solution.py:139
  388.3 4.2 %copy.95 = bf16[1,360,8,360]{1,3,2,0:T(8,128)(2,1)} copy(bf16[1,360,8,360]{3,1,2,0:T(8,128)(2,1)} %bitcast.31) | data formatting | bytes 4147200 | tf_op jit(solution)/shard_map/all_to_all | solution.py:68
  392.5 4.1 %copy.96 = bf16[1,2880,360]{1,2,0:T(8,128)(2,1)} copy(bf16[1,2880,360]{2,1,0:T(8,128)(2,1)} %bitcast.100) | data formatting | bytes 4147200
  396.6 4.1 %copy.97 = bf16[1,2880,360]{1,2,0:T(8,128)(2,1)} copy(bf16[1,2880,360]{2,1,0:T(8,128)(2,1)} %bitcast.101) | data formatting | bytes 4147200
  400.7 4.1 %copy.98 = bf16[1,360,2880]{2,1,0:T(8,128)(2,1)} copy(bf16[1,360,2880]{1,2,0:T(8,128)(2,1)} %bitcast.106) | data formatting | bytes 4147200
  404.9 0.9 fusion.4
  (63 shorter events, 8.8 us)
Async XLA Ops:
  7.2 39.9 %copy-start = (bf16[512,2880]{0,1:T(8,128)(2,1)S(1)}, bf16[512,2880]{0,1:T(8,128)(2,1)}, u32[]{:S(2)}) copy-start(bf16[512,2880]{0,1:T(8,128)(2,1)} %param.17) | copy-start | bytes 8847364
  7.2 74.6 %all-reduce.3.cloned.1.call-start = ((), (), s32[]{:S(2)}) async-start(), calls=%async_computation.8 | async-start | bytes 188416 | tf_op jit(solution)/shard_map/psum | solution.py:107
  15.1 1.0 copy-start.2
  46.7 1.8 copy-start.5
  46.7 1.8 copy-start.6
  46.8 36.0 %copy-start.4 = (f32[2880]{0:T(1024)S(1)}, f32[2880]{0:T(1024)}, u32[]{:S(2)}) copy-start(f32[2880]{0:T(1024)} %param.18) | copy-start | bytes 34564
  84.8 13.2 %all-to-all-start = ((bf16[8,4,2880]{2,1,0:T(4,128)(2,1)}), bf16[8,4,2880]{2,1,0:T(4,128)(2,1)S(1)}, u32[]{:S(2)}, u32[]{:S(2)}) async-start(bf16[8,4,2880]{2,1,0:T(4,128)(2,1)} %copy.80), calls=%async_computation | async-start | bytes 376832 | tf_op jit(solution)/shard_map/all_to_all | solution.py:128
  98.0 31.4 %all-to-all-start.1 = ((bf16[2,360,1440]{1,0,2:T(2,128)(2,1)}), bf16[2,360,1440]{1,0,2:T(2,128)(2,1)}, u32[]{:S(2)}, u32[]{:S(2)}) async-start(bf16[2,360,1440]{1,0,2:T(2,128)(2,1)} %copy.81), calls=%async_computation.1 | async-start | bytes 4423680 | tf_op jit(solution)/shard_map/all_to_all | solution.py:54
  129.5 31.4 %all-to-all-start.3 = ((bf16[2,360,1440]{1,0,2:T(2,128)(2,1)}), bf16[2,360,1440]{1,0,2:T(2,128)(2,1)}, u32[]{:S(2)}, u32[]{:S(2)}) async-start(bf16[2,360,1440]{1,0,2:T(2,128)(2,1)} %copy.84), calls=%async_computation.3 | async-start | bytes 4423680 | tf_op jit(solution)/shard_map/all_to_all | solution.py:61
  160.9 31.4 %all-to-all-start.5 = ((bf16[2,1440,360]{2,0,1:T(2,128)(2,1)}), bf16[2,1440,360]{2,0,1:T(2,128)(2,1)}, u32[]{:S(2)}, u32[]{:S(2)}) async-start(bf16[2,1440,360]{2,0,1:T(2,128)(2,1)} %copy.87), calls=%async_computation.5 | async-start | bytes 4423680 | tf_op jit(solution)/shard_map/all_to_all | solution.py:69
  192.3 55.6 %all-to-all-start.2 = ((bf16[8,360,360]{1,2,0:T(8,128)(2,1)}), bf16[8,360,360]{1,2,0:T(8,128)(2,1)}, u32[]{:S(2)}, u32[]{:S(2)}) async-start(bf16[8,360,360]{1,2,0:T(8,128)(2,1)} %bitcast.104), calls=%async_computation.2 | async-start | bytes 4423680 | tf_op jit(solution)/shard_map/all_to_all | solution.py:53
  247.9 54.6 %all-to-all-start.4 = ((bf16[8,360,360]{1,2,0:T(8,128)(2,1)}), bf16[8,360,360]{1,2,0:T(8,128)(2,1)}, u32[]{:S(2)}, u32[]{:S(2)}) async-start(bf16[8,360,360]{1,2,0:T(8,128)(2,1)} %bitcast.105), calls=%async_computation.4 | async-start | bytes 4423680 | tf_op jit(solution)/shard_map/all_to_all | solution.py:60
  302.6 54.7 %all-to-all-start.6 = ((bf16[8,360,360]{2,1,0:T(8,128)(2,1)}), bf16[8,360,360]{2,1,0:T(8,128)(2,1)}, u32[]{:S(2)}, u32[]{:S(2)}) async-start(bf16[8,360,360]{2,1,0:T(8,128)(2,1)} %bitcast.103), calls=%async_computation.6 | async-start | bytes 4423680 | tf_op jit(solution)/shard_map/all_to_all | solution.py:68
  315.6 2.3 copy-start.1
  365.4 22.8 %copy-start.3 = (f32[8,2880]{1,0:T(8,128)S(1)}, f32[8,2880]{1,0:T(8,128)}, u32[]{:S(2)}) copy-start(f32[8,2880]{1,0:T(8,128)} %all-reduce.3.cloned.1.call-done) | copy-start | bytes 276484
  383.9 20.9 %all-to-all-start.7 = ((bf16[8,4,2880]{2,1,0:T(4,128)(2,1)}), bf16[8,4,2880]{2,1,0:T(4,128)(2,1)S(1)}, u32[]{:S(2)}, u32[]{:S(2)}) async-start(bf16[8,4,2880]{2,1,0:T(4,128)(2,1)} %copy.91), calls=%async_computation.7 | async-start | bytes 376832 | tf_op jit(solution)/shard_map/all_to_all | solution.py:139
Sparse Core Ops, SparseCore 0:
  48.7 33.0 all-reduce.2
where the time goes:
time: 415 us; the launch traced here: 413 us
  waiting for transfers between devices  225 us (54%)
  local copies, waits for them, and re-layouts  85.2 us (21%)
  starting transfers between devices  37.3 us (9%)
  blocking collectives  33.2 us (8%)
  between operations  14.3 us (3%)
  matrix products  12.3 us (3%)
  other arithmetic  5.74 us (1%)
    unnamed x22, local copies, waits for them, and re-layouts  47.8 us
    all_to_all x1, waiting for transfers between devices, shards(): lax.all_to_all(lax.all_to_all(w_gate, 'cache', split_axis=2, concat_axis=...  47.1 us
    all_to_all x1, waiting for transfers between devices, shards(): lax.all_to_all(lax.all_to_all(w_up, 'cache', split_axis=2, concat_axis=0,...  46.9 us
    all_to_all x1, waiting for transfers between devices, shards(): lax.all_to_all(lax.all_to_all(w_down, 'cache', split_axis=1, concat_axis=...  38.9 us
    psum x1, waiting for transfers between devices, shards(): attention = lax.psum(projected, 'cache')  32.8 us
    all_to_all x1, waiting for transfers between devices, shards(): lax.all_to_all(w_down, 'cache', split_axis=1, concat_axis=0, tiled=True)  23.6 us
    all_to_all x1, waiting for transfers between devices, shards(): lax.all_to_all(w_gate, 'cache', split_axis=2, concat_axis=0, tiled=True)  20.2 us
    all_gather x3, blocking collectives, joined(): gathered = jax.tree.map(lambda a: lax.all_gather(a, axis), part)  18.5 us
  transfers between devices with their start and end apart: 9, of which 8 were waited for; matrix products, arithmetic and copies ran while one was open for 16% of the time, Pallas kernels for 0%

commit v1 on v0

--- a/solution.py
+++ b/solution.py
@@ -1,8 +1,11 @@
+import functools
 import math
 
 import jax
 import jax.numpy as jnp
 from jax import lax
+from jax.experimental import pallas as pl
+from jax.experimental.pallas import tpu as pltpu
 from jax.sharding import PartitionSpec as P
 
 D = 2880
@@ -10,6 +13,219 @@
 KVH = 4
 HD = 64
 TOP = 4
+
+MESH = pl.DeviceIdType.MESH
+
+
+def exchange_kernel(
+    C, E, I, wg_hbm, wu_hbm, wd_hbm, go_hbm, uo_hbm, do_hbm,
+    g_in, u_in, d_in, g_stage, u_stage, g_relay, u_relay, d_relay, g_own, u_own, d_recv, d_own,
+    load_sem, send1, recv1, send2, recv2, local_sem, out_sem,
+):
+    c = lax.axis_index("cache")
+    e = lax.axis_index("expert")
+    rows = g_own.shape[1]
+    width = g_own.shape[2]
+
+    loads = [
+        pltpu.make_async_copy(wd_hbm, d_in, load_sem.at[0]),
+        pltpu.make_async_copy(wg_hbm, g_in, load_sem.at[1]),
+        pltpu.make_async_copy(wu_hbm, u_in, load_sem.at[2]),
+    ]
+    for load in loads:
+        load.start()
+
+    barrier = pltpu.get_barrier_semaphore()
+    for k in range(1, C):
+        pl.semaphore_signal(barrier, inc=1, device_id=(lax.rem(c + k, C), e), device_id_type=MESH)
+    for k in range(1, E):
+        pl.semaphore_signal(barrier, inc=1, device_id=(c, lax.rem(e + k, E)), device_id_type=MESH)
+    pl.semaphore_wait(barrier, C - 1 + E - 1)
+
+    relays = (d_relay, g_relay, u_relay)
+    finals = (d_recv, g_own, u_own)
+
+    def own_part(w, target, i):
+        if w == 0:
+            return d_in.at[i, target]
+        return (g_stage, u_stage)[w - 1].at[target, i]
+
+    def first(w, k, i):
+        target = lax.rem(c + k, C)
+        return pltpu.make_async_remote_copy(
+            src_ref=own_part(w, target, i),
+            dst_ref=relays[w].at[c, i],
+            send_sem=send1.at[w, target, i],
+            recv_sem=recv1.at[w, c, i],
+            device_id=(target, e),
+            device_id_type=MESH,
+        )
+
+    def first_arrived(w, source, i):
+        pltpu.make_async_remote_copy(
+            src_ref=relays[w].at[source, i],
+            dst_ref=relays[w].at[source, i],
+            send_sem=send1.at[w, source, i],
+            recv_sem=recv1.at[w, source, i],
+            device_id=(source, e),
+            device_id_type=MESH,
+        ).wait_recv()
+
+    def second_ref(w, k, i):
+        source = lax.rem(c + C - k, C)
+        owner = source * I + i
+        part = own_part(w, c, i) if k == 0 else relays[w].at[source, i]
+        return source, owner, part
+
+    def second(w, k, i, action):
+        source, owner, part = second_ref(w, k, i)
+
+        @pl.when(owner != e)
+        def _():
+            copy = pltpu.make_async_remote_copy(
+                src_ref=part,
+                dst_ref=finals[w].at[e],
+                send_sem=send2.at[w, source, i],
+                recv_sem=recv2.at[w, e],
+                device_id=(c, owner),
+                device_id_type=MESH,
+            )
+            if action == "start":
+                copy.start()
+            else:
+                copy.wait_send()
+
+        @pl.when(owner == e)
+        def _():
+            copy = pltpu.make_async_copy(part, finals[w].at[e], local_sem.at[w])
+            if action == "start":
+                copy.start()
+            else:
+                copy.wait()
+
+    order = [k for k in range(2, C)] + [1] if C > 2 else list(range(1, C))
+    for w in range(3):
+        loads[w].wait()
+        for i in range(I):
+            if w > 0:
+                source = (g_in, u_in)[w - 1]
+                stage = (g_stage, u_stage)[w - 1]
+                for target in range(C):
+                    stage[target, i] = source[i, :, target * width : (target + 1) * width]
+            for k in order:
+                first(w, k, i).start()
+        for i in range(I):
+            second(w, 0, i, "start")
+    for w in range(3):
+        for i in range(I):
+            for k in [1] + order[:-1]:
+                first_arrived(w, lax.rem(c + C - k, C), i)
+                second(w, k, i, "start")
+    outs = []
+    for w in range(3):
+        for k in range(C):
+            for i in range(I):
+                second(w, k, i, "wait")
+        for k in range(1, E):
+            source = lax.rem(e + k, E)
+            pltpu.make_async_remote_copy(
+                src_ref=finals[w].at[source],
+                dst_ref=finals[w].at[source],
+                send_sem=send2.at[w, 0, 0],
+                recv_sem=recv2.at[w, source],
+                device_id=(c, source),
+                device_id_type=MESH,
+            ).wait_recv()
+        if w == 0:
+            chunk = 8 * max(n for n in range(1, 16) if d_own.shape[0] % (8 * n) == 0)
+
+            def assemble(t, carry):
+                span = pl.ds(pl.multiple_of(t * chunk, chunk), chunk)
+                d_own[span, :] = jnp.concatenate([d_recv[s, span, :] for s in range(E)], axis=-1)
+                return carry
+
+            lax.fori_loop(0, d_own.shape[0] // chunk, assemble, 0)
+            done = pltpu.make_async_copy(d_own, do_hbm, out_sem.at[0])
+        else:
+            done = pltpu.make_async_copy(finals[w], (go_hbm, uo_hbm)[w - 1], out_sem.at[w])
+        done.start()
+        outs.append(done)
+    for w in range(3):
+        for i in range(I):
+            for k in range(1, C):
+                first(w, k, i).wait_send()
+    for done in outs:
+        done.wait()
+
+
+def exchange(w_gate, w_up, w_down):
+    C = lax.axis_size("cache")
+    E = lax.axis_size("expert")
+    I, rows, hidden_width = w_gate.shape
+    width = hidden_width // C
+    bf16 = jnp.bfloat16
+    shape = jax.ShapeDtypeStruct
+    any_spec = pl.BlockSpec(memory_space=pl.ANY)
+    gate, up, down = pl.pallas_call(
+        functools.partial(exchange_kernel, C, E, I),
+        out_shape=(
+            shape((E, rows, width), bf16),
+            shape((E, rows, width), bf16),
+            shape((width, E * rows), bf16),
+        ),
+        in_specs=[any_spec] * 3,
+        out_specs=(any_spec,) * 3,
+        scratch_shapes=[
+            pltpu.VMEM((I, rows, hidden_width), bf16),
+            pltpu.VMEM((I, rows, hidden_width), bf16),
+            pltpu.VMEM((I, C, width, rows), bf16),
+            pltpu.VMEM((C, I, rows, width), bf16),
+            pltpu.VMEM((C, I, rows, width), bf16),
+            pltpu.VMEM((C, I, rows, width), bf16),
+            pltpu.VMEM((C, I, rows, width), bf16),
+            pltpu.VMEM((C, I, width, rows), bf16),
+            pltpu.VMEM((E, rows, width), bf16),
+            pltpu.VMEM((E, rows, width), bf16),
+            pltpu.VMEM((E, width, rows), bf16),
+            pltpu.VMEM((width, E * rows), bf16),
+            pltpu.SemaphoreType.DMA((3,)),
+            pltpu.SemaphoreType.DMA((3, C, I)),
+            pltpu.SemaphoreType.DMA((3, C, I)),
+            pltpu.SemaphoreType.DMA((3, C, I)),
+            pltpu.SemaphoreType.DMA((3, E)),
+            pltpu.SemaphoreType.DMA((3,)),
+            pltpu.SemaphoreType.DMA((3,)),
+        ],
+        compiler_params=pltpu.CompilerParams(
+            collective_id=0, has_side_effects=True, vmem_limit_bytes=60 << 20
+        ),
+    )(w_gate, w_up, w_down.reshape(I, C, width, rows))
+    return (
+        gate.reshape(1, E * rows, width),
+        up.reshape(1, E * rows, width),
+        down.reshape(1, width, E * rows),
+    )
+
+
+def exchange_plain(w_gate, w_up, w_down):
+    gate_owner, up_owner = (
+        lax.all_to_all(
+            lax.all_to_all(w, "cache", split_axis=2, concat_axis=0, tiled=True),
+            "expert",
+            split_axis=0,
+            concat_axis=1,
+            tiled=True,
+        )
+        for w in (w_gate, w_up)
+    )
+    down_owner = lax.all_to_all(
+        lax.all_to_all(w_down, "cache", split_axis=1, concat_axis=0, tiled=True),
+        "expert",
+        split_axis=0,
+        concat_axis=2,
+        tiled=True,
+    )
+    return gate_owner, up_owner, down_owner
 
 
 def joined(part, axis, combine):
@@ -49,29 +265,9 @@
     expert_ids,
     gate_weights,
 ):
-    gate_owner, up_owner = (
-        lax.all_to_all(
-            lax.all_to_all(w_gate, "cache", split_axis=2, concat_axis=0, tiled=True),
-            "expert",
-            split_axis=0,
-            concat_axis=1,
-            tiled=True,
-        ),
-        lax.all_to_all(
-            lax.all_to_all(w_up, "cache", split_axis=2, concat_axis=0, tiled=True),
-            "expert",
-            split_axis=0,
-            concat_axis=1,
-            tiled=True,
-        ),
-    )
-    down_owner = lax.all_to_all(
-        lax.all_to_all(w_down, "cache", split_axis=1, concat_axis=0, tiled=True),
-        "expert",
-        split_axis=0,
-        concat_axis=2,
-        tiled=True,
-    )
+    rows_local, hidden_local = w_gate.shape[1], w_gate.shape[2] // lax.axis_size("cache")
+    fits = rows_local % 8 == 0 and hidden_local % 8 == 0 and w_gate.shape[0] * lax.axis_size("cache") == lax.axis_size("expert")
+    gate_owner, up_owner, down_owner = (exchange if fits else exchange_plain)(w_gate, w_up, w_down)
     cache_count = lax.axis_size("cache")
     cache_place = lax.axis_index("cache")
     step_count = queries.shape[0]

time: 415 us -> 294 us (0.71)
  waiting for transfers between devices: 225 us -> 32.9 us
  Pallas kernels: 0 us -> 114 us
  local copies, waits for them, and re-layouts: 85.2 us -> 26.2 us
  blocking collectives: 33.2 us -> 68.2 us
  starting transfers between devices: 37.3 us -> 18.9 us
    all_to_all x6 -> x0, waiting for transfers between devices: 191 us -> none  [the longest x1 47.1 us: shards(): lax.all_to_all(lax.all_to_all(w_gate, 'cache', split_axis=2, concat_axis=...]
    pallas_call x0 -> x1, Pallas kernels: none -> 114 us  [exchange(): pl.pallas_call(functools.partial(exchange_kernel, C, E, I), out_shape=(sh...]
    psum x1, blocking collectives: 14.8 us -> 49.7 us  [shards(): expert_out = lax.psum(partial_out, 'cache').astype(jnp.bfloat16)]
    unnamed x22 -> x17, local copies, waits for them, and re-layouts: 47.8 us -> 20.2 us
    all_to_all x6 -> x0, starting transfers between devices: 27.4 us -> none  [the longest x1 5.08 us: shards(): lax.all_to_all(lax.all_to_all(w_gate, 'cache', split_axis=2, concat_axis=...]
    all_to_all x7 -> x0, local copies, waits for them, and re-layouts: 26 us -> none  [the longest x2 7.53 us: shards(): lax.all_to_all(lax.all_to_all(w_down, 'cache', split_axis=1, concat_axis=...]
    all_to_all x1, starting transfers between devices: 4.31 us -> 13.3 us  [shards(): lax.all_to_all(expert_out, 'expert', split_axis=0, concat_axis=0, tiled=T...]
    squeeze x1 -> x0, local copies, waits for them, and re-layouts: 4.82 us -> none  [shards(): down_owner[0]]
  transfers between devices with their start and end apart: 9 -> 3, of which waited for: 8 -> 1; matrix products, arithmetic and copies ran while one was open for 16% -> 3% of each run, Pallas kernels for 0% -> 39%
where the time goes in v1:
time: 294 us; the launch traced here: 293 us
  Pallas kernels  114 us (39%)
  blocking collectives  68.2 us (23%)
  waiting for transfers between devices  32.9 us (11%)
  local copies, waits for them, and re-layouts  26.2 us (9%)
  starting transfers between devices  18.9 us (6%)
  between operations  14.2 us (5%)
  matrix products  13.7 us (5%)
  other arithmetic  5.73 us (2%)
    pallas_call x1, Pallas kernels, exchange(): pl.pallas_call(functools.partial(exchange_kernel, C, E, I), out_shape=(sh...  114 us
    psum x1, blocking collectives, shards(): expert_out = lax.psum(partial_out, 'cache').astype(jnp.bfloat16)  49.7 us
    psum x1, waiting for transfers between devices, shards(): attention = lax.psum(projected, 'cache')  32.8 us
    unnamed x17, local copies, waits for them, and re-layouts  20.2 us
    all_gather x3, blocking collectives, joined(): gathered = jax.tree.map(lambda a: lax.all_gather(a, axis), part)  18.5 us
    all_to_all x1, starting transfers between devices, shards(): lax.all_to_all(expert_out, 'expert', split_axis=0, concat_axis=0, tiled=T...  13.3 us
  transfers between devices with their start and end apart: 3, of which 1 were waited for; matrix products, arithmetic and copies ran while one was open for 3% of the time, Pallas kernels for 39%

profile of v1, /device:TPU:0, one launch (start us, length us, event | category | flops | bytes accessed | tf_op | source)
XLA Modules:
  0.0 293.5 jit_solution(12197205797607449400)
XLA Ops:
  7.2 0.9 add_add_fusion
  8.1 0.9 reshape.113
  9.0 4.0 %copy.50 = bf16[4,1024,256]{1,2,0:T(8,128)(2,1)} copy(bf16[4,1024,256]{2,1,0:T(8,128)(2,1)} %param.14) | data formatting | bytes 4194304 | tf_op args[1]
  12.9 0.1 broadcast_compare_fusion
  13.0 2.1 select_reduce_fusion
  15.1 0.9 copy-done.1
  16.1 0.4 fusion.9
  16.5 6.7 %all_gather.10 = f32[4,2,4,32]{3,2,1,0:T(4,128)} all-gather(f32[1,2,4,32]{3,2,1,0:T(4,128)S(1)} %all_gather_reshape.10), channel_id=1, replica_groups=mesh['cache'=4,'expert'=8] {'cache'}, dimensions={0}, use_global_device_ids=true | all-gather | bytes 5120 | tf_op jit(solution)/shard_map/all_gather | solution.py:232
  23.2 0.7 slice_bitcast_fusion.1
  24.0 5.8 %all_gather.9 = f32[4,2,4,32]{3,2,1,0:T(4,128)} all-gather(f32[1,2,4,32]{3,2,1,0:T(4,128)S(1)} %all_gather_reshape.9), channel_id=1, replica_groups=mesh['cache'=4,'expert'=8] {'cache'}, dimensions={0}, use_global_device_ids=true | all-gather | bytes 5120 | tf_op jit(solution)/shard_map/all_gather | solution.py:232
  29.8 0.7 slice_bitcast_fusion.2
  30.5 3.9 %copy.54 = bf16[4,1024,256]{1,2,0:T(8,128)(2,1)} copy(bf16[4,1024,256]{2,1,0:T(8,128)(2,1)} %param.15) | data formatting | bytes 4194304 | tf_op args[2]
  34.4 2.6 convolution_bitcast_fusion.1
  37.1 0.1 all_gather_reshape.11
  37.2 6.0 %all_gather.11 = f32[4,2,4,2048]{3,2,1,0:T(4,128)S(1)} all-gather(f32[1,2,4,2048]{3,2,1,0:T(4,128)S(1)} %all_gather_reshape.11), channel_id=1, replica_groups=mesh['cache'=4,'expert'=8] {'cache'}, dimensions={0}, use_global_device_ids=true | all-gather | bytes 327680 | tf_op jit(solution)/shard_map/all_gather | solution.py:232
  43.2 3.6 %while.19 = (s32[]{:T(128)}, f32[2,4,32]{2,1,0:T(4,128)S(1)}, f32[2,4,32]{2,1,0:T(4,128)S(1)}, f32[2,4,2048]{2,1,0:T(4,128)S(1)}, f32[4,2,4,32]{3,2,1,0:T(4,128)...) while((s32[]{:T(128)}, f32[2,4,32]{2,1,0:T(4,128)S(1)}, ...), condition=%wide.region_3.4_spmd, body=%wide.region_2.3_spmd.sunk | while | flops 50693 | bytes 731279 | solution.py:237
  43.2 0.7 fusion.57
  44.0 0.1 reshape.135
  44.1 0.1 broadcast_in_dim.75
  44.2 0.1 reshape.136
  44.3 0.7 fusion.57
  45.2 0.1 reshape.135
  45.3 0.1 broadcast_in_dim.75
  45.4 0.1 reshape.136
  45.5 0.7 fusion.57
  46.3 0.1 reshape.135
  46.5 0.1 broadcast_in_dim.75
  46.6 0.1 reshape.136
  46.9 0.1 reshape.115
  47.0 1.5 fusion.42
  48.6 0.1 select_reduce_fusion.1
  48.7 0.2 convolution_bitcast_fusion.2
  48.9 32.8 %all-reduce.3.cloned.1.call-done = f32[8,2880]{1,0:T(8,128)} async-done(((f32[8,2880]{1,0:T(8,128)}), f32[8,2880]{1,0:T(8,128)}) %all-reduce.3.cloned.1.call-update) | async-done | bytes 92176 | tf_op jit(solution)/shard_map/psum | solution.py:303
  81.7 1.0 multiply_reduce_fusion
  82.8 1.0 multiply_convert_fusion
  83.8 0.2 convolution_convert_fusion
  84.0 0.7 copy.56
  84.8 5.5 %all-to-all-start = ((bf16[8,4,2880]{2,1,0:T(4,128)(2,1)}), bf16[8,4,2880]{2,1,0:T(4,128)(2,1)S(1)}, u32[]{:S(2)}, u32[]{:S(2)}) async-start(bf16[8,4,2880]{2,1,0:T(4,128)(2,1)} %copy.56), calls=%async_computation | async-start | bytes 376832 | tf_op jit(solution)/shard_map/all_to_all | solution.py:324
  90.3 113.6 %shard_map.138 = (bf16[8,360,360]{2,1,0:T(8,128)(2,1)}, bf16[8,360,360]{2,1,0:T(8,128)(2,1)}, bf16[360,2880]{1,0:T(8,128)(2,1)}) custom-call(bf16[2,360,1440]{2,1,0:T(8,128)(2,1)} %wg_hbm.1, bf16[2,360,1440]{2,1,0:T(8,128)(2,1)} %wu_hbm.1, bf16[2,4,360,360]{3,2,1,0:T(8,128)(2,1)} %bitcast.90), custom_call_target="tpu_custom_call" | custom-call | tf_op jit(solution)/shard_map/pallas_call | solution.py:169
  204.0 2.1 fusion.43
  206.1 4.0 %fusion.7 = f32[32,2880]{1,0:T(8,128)} fusion(bf16[360,2880]{1,0:T(8,128)(2,1)} %get-tuple-element.188, bf16[32,2880]{1,0:T(8,128)(2,1)S(1)} %reshape.120, bf16[2880,360]{1,0:T(8,128)(2,1)} %bitcast.85, f32[32,360]{1,0:T(8,128)S(1)} %fusion.43), kind=kOutput, calls=%fused_computation.17 | convolution fusion | flops 132779520 | bytes 4746240 | tf_op jit(solution)/shard_map/dot_general | solution.py:331
  210.1 1.1 reshape.122
  211.2 49.7 %all-reduce.4 = bf16[8,4,2880]{2,1,0:T(4,128)(2,1)} all-reduce(f32[8,4,2880]{2,1,0:T(4,128)S(1)} %reshape.122), channel_id=1, replica_groups=mesh['cache'=4,'expert'=8] {'cache'}, use_global_device_ids=true, to_apply=%region_8.9 | all-reduce | flops 92160 | bytes 552960 | tf_op jit(solution)/shard_map/psum | solution.py:334
  260.9 13.3 %all-to-all-start.1 = ((bf16[8,4,2880]{2,1,0:T(4,128)(2,1)}), bf16[8,4,2880]{2,1,0:T(4,128)(2,1)S(1)}, u32[]{:S(2)}, u32[]{:S(2)}) async-start(bf16[8,4,2880]{2,1,0:T(4,128)(2,1)} %all-reduce.4), calls=%async_computation.1 | async-start | bytes 376832 | tf_op jit(solution)/shard_map/all_to_all | solution.py:335
  274.3 4.1 %copy.59 = bf16[1,2880,360]{1,2,0:T(8,128)(2,1)} copy(bf16[1,2880,360]{2,1,0:T(8,128)(2,1)} %bitcast.86) | data formatting | bytes 4147200
  278.4 4.2 %copy.58 = bf16[1,2880,360]{1,2,0:T(8,128)(2,1)} copy(bf16[1,2880,360]{2,1,0:T(8,128)(2,1)} %bitcast.84) | data formatting | bytes 4147200
  282.6 0.9 fusion.4
  283.5 3.1 %copy.84 = bf16[1,360,2880]{2,1,0:T(8,128)(2,1)} copy(bf16[1,360,2880]{2,1,0:T(8,128)(2,1)} %bitcast.87) | data formatting | bytes 4147200
  (37 shorter events, 1.0 us)
Async XLA Ops:
  7.2 39.8 %copy-start = (bf16[512,2880]{0,1:T(8,128)(2,1)S(1)}, bf16[512,2880]{0,1:T(8,128)(2,1)}, u32[]{:S(2)}) copy-start(bf16[512,2880]{0,1:T(8,128)(2,1)} %param.17) | copy-start | bytes 8847364
  7.2 74.5 %all-reduce.3.cloned.1.call-start = ((), (), s32[]{:S(2)}) async-start(), calls=%async_computation.2 | async-start | bytes 188416 | tf_op jit(solution)/shard_map/psum | solution.py:303
  15.1 1.0 copy-start.1
  46.7 1.8 copy-start.4
  46.7 1.8 copy-start.5
  46.7 36.0 %copy-start.3 = (f32[2880]{0:T(1024)S(1)}, f32[2880]{0:T(1024)}, u32[]{:S(2)}) copy-start(f32[2880]{0:T(1024)} %param.18) | copy-start | bytes 34564
  84.8 119.2 %all-to-all-start = ((bf16[8,4,2880]{2,1,0:T(4,128)(2,1)}), bf16[8,4,2880]{2,1,0:T(4,128)(2,1)S(1)}, u32[]{:S(2)}, u32[]{:S(2)}) async-start(bf16[8,4,2880]{2,1,0:T(4,128)(2,1)} %copy.56), calls=%async_computation | async-start | bytes 376832 | tf_op jit(solution)/shard_map/all_to_all | solution.py:324
  260.9 21.6 %all-to-all-start.1 = ((bf16[8,4,2880]{2,1,0:T(4,128)(2,1)}), bf16[8,4,2880]{2,1,0:T(4,128)(2,1)S(1)}, u32[]{:S(2)}, u32[]{:S(2)}) async-start(bf16[8,4,2880]{2,1,0:T(4,128)(2,1)} %all-reduce.4), calls=%async_computation.1 | async-start | bytes 376832 | tf_op jit(solution)/shard_map/all_to_all | solution.py:335
  278.4 4.2 %copy-start.2 = (f32[8,2880]{1,0:T(8,128)S(1)}, f32[8,2880]{1,0:T(8,128)}, u32[]{:S(2)}) copy-start(f32[8,2880]{1,0:T(8,128)} %all-reduce.3.cloned.1.call-done) | copy-start | bytes 276484
Sparse Core Ops, SparseCore 0:
  48.7 33.0 all-reduce.2

commit v2 on v1

--- a/solution.py
+++ b/solution.py
@@ -228,30 +228,6 @@
     return gate_owner, up_owner, down_owner
 
 
-def joined(part, axis, combine):
-    gathered = jax.tree.map(lambda a: lax.all_gather(a, axis), part)
-
-    def take(source):
-        return jax.tree.map(lambda a: lax.dynamic_index_in_dim(a, source, 0, False), gathered)
-
-    return lax.fori_loop(
-        1, lax.axis_size(axis), lambda source, state: combine(state, take(source)), take(0)
-    )
-
-
-def merge_partials(first, second):
-    first_high, first_mass, first_accum = first
-    second_high, second_mass, second_accum = second
-    shared = jnp.maximum(first_high, second_high)
-    first_factor = jnp.exp(first_high - shared)
-    second_factor = jnp.exp(second_high - shared)
-    head_width = first_accum.shape[-1] // first_high.shape[-1]
-    accum = first_accum * jnp.repeat(first_factor, head_width, axis=-1) + second_accum * jnp.repeat(
-        second_factor, head_width, axis=-1
-    )
-    return (shared, first_mass * first_factor + second_mass * second_factor, accum)
-
-
 def shards(
     queries,
     k_cache,
@@ -295,12 +271,17 @@
     accum = accum.reshape(step_count, row_count, QH * HD)
     highest = highest.reshape(step_count, row_count, QH)
     own_width = w_out.shape[0]
-    all_high, all_mass, all_accum = joined((highest, mass, accum), "cache", merge_partials)
-    heads_out = all_accum / jnp.repeat(all_mass, HD, axis=-1)
-    own_out = lax.dynamic_slice_in_dim(heads_out, cache_place * own_width, own_width, 2)
+    gathered = lax.all_gather(jnp.concatenate((accum, highest, mass), axis=-1), "cache")
+    own_heads = own_width // HD
+    all_high = gathered[..., QH * HD : QH * HD + QH]
+    factor = jnp.exp(all_high - jnp.max(all_high, axis=0))
+    all_mass = jnp.sum(gathered[..., QH * HD + QH :] * factor, axis=0)
+    own_factor = lax.dynamic_slice_in_dim(factor / all_mass, cache_place * own_heads, own_heads, 3)
+    own_accum = lax.dynamic_slice_in_dim(gathered, cache_place * own_width, own_width, 3)
+    own_out = jnp.sum(own_accum * jnp.repeat(own_factor, HD, axis=-1), axis=0)
     own_rows = own_out.astype(jnp.bfloat16).reshape(step_count * row_count, own_width)
     projected = jnp.dot(own_rows, w_out, preferred_element_type=jnp.float32)
-    attention = lax.psum(projected, "cache")
+    attention = jnp.sum(lax.all_gather(projected, "cache"), axis=0)
     scale = lax.rsqrt(jnp.mean(attention * attention, axis=-1, keepdims=True) + 1e-05)
     normed = (attention * scale * norm_gain).astype(jnp.bfloat16).reshape(step_count, row_count, D)
     experts_total = w_gate.shape[0] * cache_count
@@ -331,7 +312,7 @@
     partial_out = jnp.dot(hidden, down_owner[0], preferred_element_type=jnp.float32).reshape(
         source_count, item_count, D
     )
-    expert_out = lax.psum(partial_out, "cache").astype(jnp.bfloat16)
+    expert_out = partial_out.astype(jnp.bfloat16)
     returned = lax.all_to_all(expert_out, "expert", split_axis=0, concat_axis=0, tiled=True)
     back_width = returned.shape[-1]
     returned = returned.reshape(experts_total, step_count, capacity, back_width)
@@ -342,6 +323,7 @@
         precision=lax.Precision.HIGHEST,
     )
     attention_rows = attention.reshape(step_count, row_count, D)
+    combined = jnp.sum(lax.all_gather(combined, "cache"), axis=0)
     mixed = (attention_rows + combined).astype(jnp.bfloat16)
     return (mixed, gate_owner, up_owner, down_owner)
 

time: 294 us -> 231 us (0.79)
  blocking collectives: 68.2 us -> 19.9 us
  starting transfers between devices: 18.9 us -> 55 us
  waiting for transfers between devices: 32.9 us -> 0.01 us
  between operations: 14.2 us -> 0.83 us
  other arithmetic: 5.73 us -> 2.62 us
  Pallas kernels: 114 us -> 117 us
    psum x1 -> x0, blocking collectives: 49.7 us -> none  [shards(): expert_out = lax.psum(partial_out, 'cache').astype(jnp.bfloat16)]
    all_to_all x1, starting transfers between devices: 13.3 us -> 49.2 us  [shards(): lax.all_to_all(expert_out, 'expert', split_axis=0, concat_axis=0, tiled=T...]
    psum x1 -> x0, waiting for transfers between devices: 32.8 us -> none  [shards(): attention = lax.psum(projected, 'cache')]
    pallas_call x1, Pallas kernels: 114 us -> 117 us  [exchange(): pl.pallas_call(functools.partial(exchange_kernel, C, E, I), out_shape=(sh...]
    unnamed x17 -> x15, local copies, waits for them, and re-layouts: 20.2 us -> 20.2 us
  transfers between devices with their start and end apart: 3 -> 2, of which waited for: 1 -> 0; matrix products, arithmetic and copies ran while one was open for 3% -> 4% of each run, Pallas kernels for 39% -> 51%
where the time goes in v2:
time: 231 us; the launch traced here: 230 us
  Pallas kernels  117 us (51%)
  starting transfers between devices  55 us (24%)
  local copies, waits for them, and re-layouts  23.5 us (10%)
  blocking collectives  19.9 us (9%)
  matrix products  11.6 us (5%)
  other arithmetic  2.62 us (1%)
    pallas_call x1, Pallas kernels, exchange(): pl.pallas_call(functools.partial(exchange_kernel, C, E, I), out_shape=(sh...  117 us
    all_to_all x1, starting transfers between devices, shards(): lax.all_to_all(expert_out, 'expert', split_axis=0, concat_axis=0, tiled=T...  49.2 us
    unnamed x15, local copies, waits for them, and re-layouts  20.2 us
    all_gather x1, blocking collectives, shards(): lax.all_gather(jnp.concatenate((accum, highest, mass), axis=-1), 'cache')  7.3 us
    all_gather x1, blocking collectives, shards(): attention = jnp.sum(lax.all_gather(projected, 'cache'), axis=0)  6.49 us
    all_gather x1, blocking collectives, shards(): combined = jnp.sum(lax.all_gather(combined, 'cache'), axis=0)  6.1 us
    all_to_all x1, starting transfers between devices, shards(): lax.all_to_all(outgoing, 'expert', split_axis=0, concat_axis=0, tiled=True)  5.83 us
  transfers between devices with their start and end apart: 2, of which 0 were waited for; matrix products, arithmetic and copies ran while one was open for 4% of the time, Pallas kernels for 51%

profile of v2, /device:TPU:0, one launch (start us, length us, event | category | flops | bytes accessed | tf_op | source)
XLA Modules:
  0.0 230.3 jit_solution(721477346633662655)
XLA Ops:
  0.6 0.0 copy-start
  0.7 0.9 add_add_fusion
  1.5 0.9 reshape.118
  2.4 4.0 %copy.49 = bf16[4,1024,256]{1,2,0:T(8,128)(2,1)} copy(bf16[4,1024,256]{2,1,0:T(8,128)(2,1)} %param.12) | data formatting | bytes 4194304 | tf_op args[1]
  6.4 0.1 broadcast_compare_fusion
  6.5 2.1 select_reduce_fusion
  8.6 0.0 copy-start.1
  8.6 0.9 copy-done.1
  9.5 0.4 fusion.2
  9.9 0.1 reshape.122
  10.0 0.1 reshape.121
  10.1 3.9 %copy.51 = bf16[4,1024,256]{1,2,0:T(8,128)(2,1)} copy(bf16[4,1024,256]{2,1,0:T(8,128)(2,1)} %param.13) | data formatting | bytes 4194304 | tf_op args[2]
  14.0 2.6 %convolution_bitcast_fusion.1 = f32[2,4,4,8,64]{4,3,0,2,1:T(8,128)S(1)} fusion(bf16[4,1024,4,64,1]{1,3,4,2,0:T(8,128)(2,1)} %bitcast.62, f32[2,4,4,8,1024]{4,3,0,2,1:T(8,128)} %copy-done.1, f32[2,4,4,8]{3,0,2,1:T(2,128)S(1)} %get-tuple-element.34, pred[2,4,1024]{2,0,1:T(4,128)(4,1)S(1)} %broadcast_compare_fusion), kind=kOutput, calls=%fused_computation.5 | convolution fusion | flops 34340864 | bytes 3220480 | tf_op jit(solution)/shard_map/srhgp,rphd->srhgd/dot_general | solution.py:265
  16.7 0.1 reshape.120
  16.8 0.1 concatenate.3
  16.9 7.3 %all-gather = f32[8,4,2112]{2,1,0:T(4,128)S(1)} all-gather(f32[2,4,2112]{2,1,0:T(4,128)S(1)} %concatenate.3), channel_id=2, replica_groups=mesh['cache'=4,'expert'=8] {'cache'}, dimensions={0}, use_global_device_ids=true | all-gather | bytes 337920 | tf_op jit(solution)/shard_map/all_gather | solution.py:274
  24.2 0.1 fusion.19
  24.3 0.1 constant_dynamic-slice_fusion
  24.3 0.1 dynamic-slice_divide_fusion
  24.4 0.1 broadcast_in_dim.23
  24.5 0.1 reshape.123
  24.6 0.1 multiply_reduce_fusion.1
  24.8 0.0 copy-start.3
  24.8 0.0 copy-start.4
  24.8 0.0 copy-start.2
  24.8 0.8 fusion.38
  25.7 6.5 %all-gather.1 = f32[32,2880]{1,0:T(8,128)S(1)} all-gather(f32[8,2880]{1,0:T(8,128)S(1)} %fusion.38), channel_id=3, replica_groups=mesh['cache'=4,'expert'=8] {'cache'}, dimensions={0}, use_global_device_ids=true | all-gather | bytes 460800 | tf_op jit(solution)/shard_map/all_gather | solution.py:284
  32.2 0.1 multiply_reduce_fusion
  32.4 0.1 rsqrt.12
  32.5 0.1 select_reduce_fusion.1
  32.6 0.2 convolution_bitcast_fusion.2
  32.8 0.3 convolution_convert_fusion.1
  33.0 0.7 copy.55
  33.8 5.8 %all-to-all-start = ((bf16[8,4,2880]{2,1,0:T(4,128)(2,1)}), bf16[8,4,2880]{2,1,0:T(4,128)(2,1)S(1)}, u32[]{:S(2)}, u32[]{:S(2)}) async-start(bf16[8,4,2880]{2,1,0:T(4,128)(2,1)} %copy.55), calls=%async_computation | async-start | bytes 376832 | tf_op jit(solution)/shard_map/all_to_all | solution.py:305
  39.6 116.9 %shard_map.138 = (bf16[8,360,360]{2,1,0:T(8,128)(2,1)}, bf16[8,360,360]{2,1,0:T(8,128)(2,1)}, bf16[360,2880]{1,0:T(8,128)(2,1)}) custom-call(bf16[2,360,1440]{2,1,0:T(8,128)(2,1)} %wg_hbm.1, bf16[2,360,1440]{2,1,0:T(8,128)(2,1)} %wu_hbm.1, bf16[2,4,360,360]{3,2,1,0:T(8,128)(2,1)} %bitcast.63), custom_call_target="tpu_custom_call" | custom-call | tf_op jit(solution)/shard_map/pallas_call | solution.py:169
  156.5 0.1 reshape.126
  156.6 2.1 fusion.39
  158.7 3.3 %convolution_convert_fusion = bf16[32,2880]{1,0:T(8,128)(2,1)S(1)} fusion(bf16[360,2880]{1,0:T(8,128)(2,1)} %get-tuple-element.9, bf16[32,2880]{1,0:T(8,128)(2,1)S(1)} %reshape.126, bf16[2880,360]{1,0:T(8,128)(2,1)} %bitcast.56, f32[32,360]{1,0:T(8,128)S(1)} %fusion.39), kind=kOutput, calls=%fused_computation | convolution fusion | flops 132871680 | bytes 4561920 | tf_op jit(solution)/shard_map/dot_general | solution.py:312
  161.9 0.7 convert_element_type.50
  162.7 49.2 %all-to-all-start.1 = ((bf16[8,4,2880]{2,1,0:T(4,128)(2,1)}), bf16[8,4,2880]{2,1,0:T(4,128)(2,1)S(1)}, u32[]{:S(2)}, u32[]{:S(2)}) async-start(bf16[8,4,2880]{2,1,0:T(4,128)(2,1)} %convert_element_type.50), calls=%async_computation.1 | async-start | bytes 376832 | tf_op jit(solution)/shard_map/all_to_all | solution.py:316
  211.8 4.1 %copy.58 = bf16[1,2880,360]{1,2,0:T(8,128)(2,1)} copy(bf16[1,2880,360]{2,1,0:T(8,128)(2,1)} %bitcast.57) | data formatting | bytes 4147200
  216.0 4.1 %copy.57 = bf16[1,2880,360]{1,2,0:T(8,128)(2,1)} copy(bf16[1,2880,360]{2,1,0:T(8,128)(2,1)} %bitcast.59) | data formatting | bytes 4147200
  220.1 0.0 all-to-all-done.1
  220.1 0.3 convolution_bitcast_fusion
  220.4 6.1 %all-gather.2 = f32[8,4,2880]{2,1,0:T(4,128)S(1)} all-gather(f32[2,4,2880]{2,1,0:T(4,128)S(1)} %convolution_bitcast_fusion), channel_id=4, replica_groups=mesh['cache'=4,'expert'=8] {'cache'}, dimensions={0}, use_global_device_ids=true | all-gather | bytes 460800 | tf_op jit(solution)/shard_map/all_gather | solution.py:326
  226.5 0.1 reduce_sum.79
  226.6 0.6 add_convert_fusion
  227.2 3.1 %copy.68 = bf16[1,360,2880]{2,1,0:T(8,128)(2,1)} copy(bf16[1,360,2880]{2,1,0:T(8,128)(2,1)} %bitcast.60) | data formatting | bytes 4147200
  (16 shorter events, 0.1 us)
Async XLA Ops:
  0.6 24.1 %copy-start = (bf16[512,2880]{0,1:T(8,128)(2,1)S(1)}, bf16[512,2880]{0,1:T(8,128)(2,1)}, u32[]{:S(2)}) copy-start(bf16[512,2880]{0,1:T(8,128)(2,1)} %param.15) | copy-start | bytes 8847364
  8.6 1.0 copy-start.1
  24.8 7.7 %copy-start.3 = (f32[2,4,4]{2,1,0:T(4,128)S(1)}, f32[2,4,4]{2,1,0:T(4,128)}, u32[]{:S(2)}) copy-start(f32[2,4,4]{2,1,0:T(4,128)} %param.21) | copy-start | bytes 388
  24.8 7.7 %copy-start.4 = (s32[2,4,4]{2,1,0:T(4,128)S(1)}, s32[2,4,4]{2,1,0:T(4,128)}, u32[]{:S(2)}) copy-start(s32[2,4,4]{2,1,0:T(4,128)} %param.20) | copy-start | bytes 388
  24.8 7.9 %copy-start.2 = (f32[2880]{0:T(1024)S(1)}, f32[2880]{0:T(1024)}, u32[]{:S(2)}) copy-start(f32[2880]{0:T(1024)} %param.16) | copy-start | bytes 34564
  33.8 122.7 %all-to-all-start = ((bf16[8,4,2880]{2,1,0:T(4,128)(2,1)}), bf16[8,4,2880]{2,1,0:T(4,128)(2,1)S(1)}, u32[]{:S(2)}, u32[]{:S(2)}) async-start(bf16[8,4,2880]{2,1,0:T(4,128)(2,1)} %copy.55), calls=%async_computation | async-start | bytes 376832 | tf_op jit(solution)/shard_map/all_to_all | solution.py:305
  162.7 57.4 %all-to-all-start.1 = ((bf16[8,4,2880]{2,1,0:T(4,128)(2,1)}), bf16[8,4,2880]{2,1,0:T(4,128)(2,1)S(1)}, u32[]{:S(2)}, u32[]{:S(2)}) async-start(bf16[8,4,2880]{2,1,0:T(4,128)(2,1)} %convert_element_type.50), calls=%async_computation.1 | async-start | bytes 376832 | tf_op jit(solution)/shard_map/all_to_all | solution.py:316

commit v3 on v2

--- a/solution.py
+++ b/solution.py
@@ -250,26 +250,36 @@
     row_count = k_cache.shape[0]
     positions = k_cache.shape[1]
     group_size = QH // KVH
-    query_heads = queries.reshape(step_count, row_count, KVH, group_size, HD)
-    key_heads = k_cache.reshape(row_count, positions, KVH, HD)
-    value_heads = v_cache.reshape(row_count, positions, KVH, HD)
+    heads = queries.reshape(step_count, row_count, KVH, group_size, HD).transpose(1, 2, 0, 3, 4)
+    same = jnp.eye(KVH, dtype=jnp.float32)
+    spread = heads[:, :, :, :, None, :] * same.astype(heads.dtype)[None, :, None, None, :, None]
+    spread = spread.reshape(row_count, step_count * QH, KVH * HD)
     scores = jnp.einsum(
-        "srhgd,rphd->srhgp", query_heads, key_heads, preferred_element_type=jnp.float32
+        "rnk,rpk->rnp", spread, k_cache, preferred_element_type=jnp.float32
     ) * (1.0 / math.sqrt(HD))
     position = cache_place * positions + jnp.arange(positions, dtype=jnp.int32)
-    limit = lengths[None, :] + jnp.arange(step_count, dtype=jnp.int32)[:, None] + 1
-    visible = (position[None, None, :] < limit[:, :, None])[:, :, None, None, :]
+    limit = lengths[:, None] + jnp.arange(step_count, dtype=jnp.int32)[None, :] + 1
+    limit = jnp.broadcast_to(
+        limit[:, None, :, None], (row_count, KVH, step_count, group_size)
+    ).reshape(row_count, step_count * QH)
+    visible = position[None, None, :] < limit[:, :, None]
     highest = jnp.max(jnp.where(visible, scores, -1e30), axis=-1)
     weights = jnp.where(visible, jnp.exp(scores - highest[..., None]), 0.0)
-    mass = jnp.sum(weights, axis=-1).reshape(step_count, row_count, QH)
+    mass = jnp.sum(weights, axis=-1)
     accum = jnp.einsum(
-        "srhgp,rphd->srhgd",
+        "rnp,rpk->rnk",
         weights.astype(jnp.bfloat16),
-        value_heads,
+        v_cache,
         preferred_element_type=jnp.float32,
-    )
-    accum = accum.reshape(step_count, row_count, QH * HD)
-    highest = highest.reshape(step_count, row_count, QH)
+    ).reshape(row_count, KVH, step_count, group_size, KVH, HD)
+    accum = jnp.sum(accum * same[None, :, None, None, :, None], axis=4)
+
+    def by_step(a):
+        return jnp.moveaxis(a, 2, 0).reshape(step_count, row_count, -1)
+
+    accum = by_step(accum)
+    highest = by_step(highest.reshape(row_count, KVH, step_count, group_size))
+    mass = by_step(mass.reshape(row_count, KVH, step_count, group_size))
     own_width = w_out.shape[0]
     gathered = lax.all_gather(jnp.concatenate((accum, highest, mass), axis=-1), "cache")
     own_heads = own_width // HD

time: 231 us -> 228 us (0.987)
  local copies, waits for them, and re-layouts: 23.5 us -> 16.7 us
    unnamed x15 -> x11, local copies, waits for them, and re-layouts: 20.2 us -> 11.4 us
  transfers between devices with their start and end apart: 2 -> 2, of which waited for: 0 -> 0; matrix products, arithmetic and copies ran while one was open for 4% -> 4% of each run, Pallas kernels for 51% -> 52%
where the time goes in v3:
time: 228 us; the launch traced here: 227 us
  Pallas kernels  117 us (51%)
  starting transfers between devices  55 us (24%)
  blocking collectives  19.9 us (9%)
  local copies, waits for them, and re-layouts  16.7 us (7%)
  matrix products  13.4 us (6%)
  other arithmetic  4.19 us (2%)
    pallas_call x1, Pallas kernels, exchange(): pl.pallas_call(functools.partial(exchange_kernel, C, E, I), out_shape=(sh...  117 us
    all_to_all x1, starting transfers between devices, shards(): lax.all_to_all(expert_out, 'expert', split_axis=0, concat_axis=0, tiled=T...  49.1 us
    unnamed x11, local copies, waits for them, and re-layouts  11.4 us
    all_gather x1, blocking collectives, shards(): lax.all_gather(jnp.concatenate((accum, highest, mass), axis=-1), 'cache')  7.3 us
    all_gather x1, blocking collectives, shards(): attention = jnp.sum(lax.all_gather(projected, 'cache'), axis=0)  6.49 us
    all_gather x1, blocking collectives, shards(): combined = jnp.sum(lax.all_gather(combined, 'cache'), axis=0)  6.1 us
    all_to_all x1, starting transfers between devices, shards(): lax.all_to_all(outgoing, 'expert', split_axis=0, concat_axis=0, tiled=True)  5.83 us
  transfers between devices with their start and end apart: 2, of which 0 were waited for; matrix products, arithmetic and copies ran while one was open for 4% of the time, Pallas kernels for 52%

profile of v3, /device:TPU:0, one launch (start us, length us, event | category | flops | bytes accessed | tf_op | source)
XLA Modules:
  0.0 226.9 jit_solution(9912708471896513911)
XLA Ops:
  0.7 0.9 add_add_fusion
  1.6 0.1 broadcast_in_dim.11
  1.6 0.1 lt.22
  1.7 0.1 mul.104
  1.8 0.1 mul.105
  1.9 0.9 reshape.145
  2.8 0.1 mul.102
  2.9 0.2 mul.103
  3.2 3.3 %fusion.1 = (f32[4,64]{1,0:T(4,128)S(1)}, f32[4,64,1024]{2,1,0:T(8,128)}) fusion(s32[4,64]{1,0:T(4,128)S(1)} %lt.22, s32[1024]{0:T(1024)S(1)} %iota_add_fusion, bf16[4,1024,256]{2,1,0:T(8,128)(2,1)} %param.12, bf16[4,64,256]{2,1,0:T(8,128)(2,1)S(1)} %mul.103, bf16[64,256]{1,0:T(8,128)(2,1)S(1)} %mul.105), kind=kOutput, calls=%fused_computation.9 | convolution fusion | flops 135331584 | bytes 3315712 | tf_op jit(solution)/shard_map/rnk,rpk->rnp/dot_general | solution.py:257
  6.5 0.1 reshape.148
  6.6 1.6 fusion.2
  8.2 3.1 %fusion.4 = f32[4,64,256]{2,1,0:T(8,128)} fusion(bf16[4,1024,256]{2,1,0:T(8,128)(2,1)} %param.13, f32[4,64,1024]{2,1,0:T(8,128)} %get-tuple-element.35, f32[4,64]{1,0:T(4,128)S(1)} %get-tuple-element.34, s32[4,64]{1,0:T(4,128)S(1)} %lt.22, s32[1024]{0:T(1024)S(1)} %iota_add_fusion), kind=kOutput, calls=%fused_computation.12 | convolution fusion | flops 135266304 | bytes 3414016 | tf_op jit(solution)/shard_map/rnp,rpk->rnk/dot_general | solution.py:269
  11.3 0.1 reshape.149
  11.4 0.1 reshape.150
  11.5 0.1 reshape.151
  11.6 1.2 reshape.146
  12.8 0.4 multiply_reduce_fusion
  13.2 0.1 reshape.147
  13.3 0.1 concatenate.3
  13.4 7.3 %all-gather = f32[8,4,2112]{2,1,0:T(4,128)S(1)} all-gather(f32[2,4,2112]{2,1,0:T(4,128)S(1)} %concatenate.3), channel_id=2, replica_groups=mesh['cache'=4,'expert'=8] {'cache'}, dimensions={0}, use_global_device_ids=true | all-gather | bytes 337920 | tf_op jit(solution)/shard_map/all_gather | solution.py:284
  20.7 0.1 fusion.22
  20.8 0.1 constant_dynamic-slice_fusion
  20.9 0.1 dynamic-slice_divide_fusion
  21.0 0.1 broadcast_in_dim.14
  21.1 0.1 reshape.152
  21.2 0.1 multiply_reduce_fusion.2
  21.4 0.8 fusion.43
  22.2 6.5 %all-gather.1 = f32[32,2880]{1,0:T(8,128)S(1)} all-gather(f32[8,2880]{1,0:T(8,128)S(1)} %fusion.43), channel_id=3, replica_groups=mesh['cache'=4,'expert'=8] {'cache'}, dimensions={0}, use_global_device_ids=true | all-gather | bytes 460800 | tf_op jit(solution)/shard_map/all_gather | solution.py:294
  28.7 0.1 multiply_reduce_fusion.1
  28.9 0.1 rsqrt.12
  29.0 0.1 select_reduce_fusion
  29.1 0.2 convolution_bitcast_fusion.1
  29.3 0.3 convolution_convert_fusion.1
  29.6 0.7 copy.44
  30.3 5.8 %all-to-all-start = ((bf16[8,4,2880]{2,1,0:T(4,128)(2,1)}), bf16[8,4,2880]{2,1,0:T(4,128)(2,1)S(1)}, u32[]{:S(2)}, u32[]{:S(2)}) async-start(bf16[8,4,2880]{2,1,0:T(4,128)(2,1)} %copy.44), calls=%async_computation | async-start | bytes 376832 | tf_op jit(solution)/shard_map/all_to_all | solution.py:315
  36.2 116.9 %shard_map.138 = (bf16[8,360,360]{2,1,0:T(8,128)(2,1)}, bf16[8,360,360]{2,1,0:T(8,128)(2,1)}, bf16[360,2880]{1,0:T(8,128)(2,1)}) custom-call(bf16[2,360,1440]{2,1,0:T(8,128)(2,1)} %wg_hbm.1, bf16[2,360,1440]{2,1,0:T(8,128)(2,1)} %wu_hbm.1, bf16[2,4,360,360]{3,2,1,0:T(8,128)(2,1)} %bitcast.51), custom_call_target="tpu_custom_call" | custom-call | tf_op jit(solution)/shard_map/pallas_call | solution.py:169
  153.1 0.1 reshape.155
  153.2 2.1 fusion.44
  155.2 3.3 %convolution_convert_fusion = bf16[32,2880]{1,0:T(8,128)(2,1)S(1)} fusion(bf16[360,2880]{1,0:T(8,128)(2,1)} %get-tuple-element.9, bf16[32,2880]{1,0:T(8,128)(2,1)S(1)} %reshape.155, bf16[2880,360]{1,0:T(8,128)(2,1)} %bitcast.46, f32[32,360]{1,0:T(8,128)S(1)} %fusion.44), kind=kOutput, calls=%fused_computation | convolution fusion | flops 132871680 | bytes 4561920 | tf_op jit(solution)/shard_map/dot_general | solution.py:322
  158.5 0.7 convert_element_type.71
  159.2 49.1 %all-to-all-start.1 = ((bf16[8,4,2880]{2,1,0:T(4,128)(2,1)}), bf16[8,4,2880]{2,1,0:T(4,128)(2,1)S(1)}, u32[]{:S(2)}, u32[]{:S(2)}) async-start(bf16[8,4,2880]{2,1,0:T(4,128)(2,1)} %convert_element_type.71), calls=%async_computation.1 | async-start | bytes 376832 | tf_op jit(solution)/shard_map/all_to_all | solution.py:326
  208.4 4.1 %copy.47 = bf16[1,2880,360]{1,2,0:T(8,128)(2,1)} copy(bf16[1,2880,360]{2,1,0:T(8,128)(2,1)} %bitcast.47) | data formatting | bytes 4147200
  212.5 4.1 %copy.46 = bf16[1,2880,360]{1,2,0:T(8,128)(2,1)} copy(bf16[1,2880,360]{2,1,0:T(8,128)(2,1)} %bitcast.49) | data formatting | bytes 4147200
  216.7 0.3 convolution_bitcast_fusion
  217.0 6.1 %all-gather.2 = f32[8,4,2880]{2,1,0:T(4,128)S(1)} all-gather(f32[2,4,2880]{2,1,0:T(4,128)S(1)} %convolution_bitcast_fusion), channel_id=4, replica_groups=mesh['cache'=4,'expert'=8] {'cache'}, dimensions={0}, use_global_device_ids=true | all-gather | bytes 460800 | tf_op jit(solution)/shard_map/all_gather | solution.py:336
  223.1 0.1 reduce_sum.89
  223.2 0.6 add_convert_fusion
  223.8 3.1 %copy.51 = bf16[1,360,2880]{2,1,0:T(8,128)(2,1)} copy(bf16[1,360,2880]{2,1,0:T(8,128)(2,1)} %bitcast.50) | data formatting | bytes 4147200
  (24 shorter events, 0.2 us)
Async XLA Ops:
  0.6 20.7 %copy-start = (bf16[512,2880]{0,1:T(8,128)(2,1)S(1)}, bf16[512,2880]{0,1:T(8,128)(2,1)}, u32[]{:S(2)}) copy-start(bf16[512,2880]{0,1:T(8,128)(2,1)} %param.15) | copy-start | bytes 8847364
  21.2 7.8 %copy-start.2 = (f32[2,4,4]{2,1,0:T(4,128)S(1)}, f32[2,4,4]{2,1,0:T(4,128)}, u32[]{:S(2)}) copy-start(f32[2,4,4]{2,1,0:T(4,128)} %param.21) | copy-start | bytes 388
  21.2 7.8 %copy-start.3 = (s32[2,4,4]{2,1,0:T(4,128)S(1)}, s32[2,4,4]{2,1,0:T(4,128)}, u32[]{:S(2)}) copy-start(s32[2,4,4]{2,1,0:T(4,128)} %param.20) | copy-start | bytes 388
  21.3 8.0 %copy-start.1 = (f32[2880]{0:T(1024)S(1)}, f32[2880]{0:T(1024)}, u32[]{:S(2)}) copy-start(f32[2880]{0:T(1024)} %param.16) | copy-start | bytes 34564
  30.3 122.7 %all-to-all-start = ((bf16[8,4,2880]{2,1,0:T(4,128)(2,1)}), bf16[8,4,2880]{2,1,0:T(4,128)(2,1)S(1)}, u32[]{:S(2)}, u32[]{:S(2)}) async-start(bf16[8,4,2880]{2,1,0:T(4,128)(2,1)} %copy.44), calls=%async_computation | async-start | bytes 376832 | tf_op jit(solution)/shard_map/all_to_all | solution.py:315
  159.2 57.4 %all-to-all-start.1 = ((bf16[8,4,2880]{2,1,0:T(4,128)(2,1)}), bf16[8,4,2880]{2,1,0:T(4,128)(2,1)S(1)}, u32[]{:S(2)}, u32[]{:S(2)}) async-start(bf16[8,4,2880]{2,1,0:T(4,128)(2,1)} %convert_element_type.71), calls=%async_computation.1 | async-start | bytes 376832 | tf_op jit(solution)/shard_map/all_to_all | solution.py:326
